TPU v7x, 64 devices: a 2x2x8 block of a 4x4x8 slice. The times are simulated.
64 devices in a mesh: dp: 4 (over x, y), tp: 16 (over z, core).
Axes of the slice: x: 2, y: 2, z: 8, core: 2. Of those that a mesh axis runs over, the one named last changes fastest.
The devices are a block of a 4x4x8 slice.
Arguments:
- hidden: bfloat16 [4, 2048, 2560], P('dp'), parts along dimension 0
- ln_gain: float32 [2560], replicated
- ln_bias: float32 [2560], replicated
- embedding: bfloat16 [51200, 2560], P('tp')
- targets: int32 [4, 2048], P('dp'), parts along dimension 0
- score_mask: int32 [4, 2048], P('dp'), parts along dimension 0
Outputs:
- output 1: float32 [4, 2048], P('dp'), parts along dimension 0
- output 2: float32 [4, 2048], P('dp'), parts along dimension 0
- output 3: float32 [4], P('dp'), parts along dimension 0
- output 4: float32 [4, 2048], P('dp'), parts along dimension 0
There are 4 independent parts. A program takes and returns all parts, laid end to end along the dimension named above; an argument that names none is the same for every part.
All inputs are finite; a program needn't handle non-finite values.
Results may differ from a plain program's by a relative error of at most 0.001.
Values sent between devices are 32-bit elements.
A program may use at most 768 MiB of HBM per device.

v0:
```python
import jax
import jax.numpy as jnp
from jax import lax
from jax.sharding import PartitionSpec as P

OPT_VOCAB = 50272
LN_EPS = 1e-5


def layer_norm(hidden, ln_gain, ln_bias):
    hidden_f = hidden.astype(jnp.float32)
    row_mean = jnp.mean(hidden_f, axis=-1, keepdims=True)
    centered = hidden_f - row_mean
    row_var = jnp.mean(centered * centered, axis=-1, keepdims=True)
    return (centered * lax.rsqrt(row_var + LN_EPS) * ln_gain + ln_bias).astype(jnp.bfloat16)


def solution(mesh):
    def local_part(hidden, ln_gain, ln_bias, embedding, targets, score_mask):
        shard_rows = embedding.shape[0]
        vocab_ids = lax.axis_index("tp") * shard_rows + jnp.arange(shard_rows)
        normed = layer_norm(hidden, ln_gain, ln_bias)
        logits = jnp.einsum("bsd,vd->bsv", normed, embedding, preferred_element_type=jnp.float32)
        logits = jnp.where(vocab_ids < OPT_VOCAB, logits, -jnp.inf)
        row_max = lax.pmax(jnp.max(logits, axis=-1), "tp")
        exp_sum = jnp.sum(jnp.exp(logits - row_max[..., None]), axis=-1)
        target_part = jnp.sum(jnp.where(vocab_ids == targets[..., None], logits, 0.0), axis=-1)
        combined = lax.psum(jnp.stack([exp_sum, target_part]), "tp")
        log_norm = row_max + jnp.log(combined[0])
        token_logp = (combined[1] - log_norm) * score_mask.astype(jnp.float32)
        return log_norm, token_logp, jnp.sum(token_logp, axis=-1), row_max - log_norm

    row_spec = P("dp", None)
    return jax.shard_map(local_part, mesh=mesh, in_specs=(P("dp", None, None), P(), P(), P("tp", None), row_spec, row_spec), out_specs=(row_spec, row_spec, P("dp"), row_spec), check_vma=False)
```

profile of v0, /device:TPU:21, one launch (start us, length us, event | category | flops | bytes accessed | tf_op | source)
XLA Modules:
  0.0 146.7 jit_solution(13357886679329675951)
XLA Ops:
  0.6 0.0 copy-start.3
  0.6 0.0 copy-start.4
  0.7 5.4 %convert_reduce_fusion = f32[2048]{0:T(1024)S(1)} fusion(bf16[1,2048,2560]{2,1,0:T(8,128)(2,1)} %param.6), kind=kLoop, calls=%fused_computation.3 | loop fusion | flops 10483712 | bytes 10493952 | tf_op jit(solution)/shard_map/reduce_sum | solution.py:12
  6.1 6.8 %fusion.2 = f32[2048]{0:T(1024)S(1)} fusion(bf16[1,2048,2560]{2,1,0:T(8,128)(2,1)} %param.6, f32[2048]{0:T(1024)S(1)} %broadcast_multiply_fusion), kind=kLoop, calls=%fused_computation.7 | loop fusion | flops 20969472 | bytes 10502144 | tf_op jit(solution)/shard_map/reduce_sum | solution.py:14
  12.9 0.0 copy-done.3
  13.0 0.0 copy-done.4
  13.0 0.0 copy-start.1
  13.0 46.6 %select_reduce_fusion.1 = (f32[2048]{0:T(1024)S(1)}, f32[2048,3200]{1,0:T(8,128)}) fusion(pred[3200]{0:T(1024)(128)(4,1)S(1)} %broadcast_compare_fusion, bf16[3200,2560]{1,0:T(8,128)(2,1)} %param.9, bf16[1,2048,2560]{2,1,0:T(8,128)(2,1)} %param.6, f32[2560]{0:T(1024)S(1)} %copy-done.3, f32[2560]{0:T(1024)S(1)} %copy-done.4, f32[2048]{0:T(1024)S(1)} %add_rsqrt_fusion, ...), kind=kOutput, calls=%fused_computation.6 | convolution fusion | flops 33598994432 | bytes 53132416 | tf_op jit(solution)/shard_map/bsd,vd->bsv/dot_general | solution.py:23
  59.5 0.0 copy-start.2
  59.5 29.3 %pmax.7 = f32[1,2048]{1,0:T(1,128)S(1)} all-reduce(f32[1,2048]{1,0:T(1,128)S(1)} %bitcast.28), channel_id=1, replica_groups=mesh['dp'=4,'tp'=16] {'tp'}, use_global_device_ids=true, to_apply=%region_3.4 | all-reduce | flops 2048 | bytes 16384 | tf_op jit(solution)/shard_map/pmax | solution.py:25
  88.8 0.0 copy-done.1
  88.8 10.7 %exponential_reduce_fusion = (f32[2048]{0:T(1024)S(1)}, f32[2048]{0:T(1024)S(1)}) fusion(f32[2048,3200]{1,0:T(8,128)} %get-tuple-element.11, f32[2048]{0:T(1024)S(1)} %bitcast.24, pred[3200]{0:T(1024)(128)(4,1)S(1)} %broadcast_compare_fusion, s32[2048]{0:T(1024)S(1)} %bitcast.27, s32[3200]{0:T(1024)S(1)} %iota_add_fusion), kind=kLoop, calls=%fused_computation.1 | loop fusion | flops 39317504 | bytes 26263168 | tf_op jit(solution)/shard_map/reduce_sum | solution.py:26
  99.6 45.2 %psum.7 = f32[2,1,2048]{2,1,0:T(1,128)S(1)} all-reduce(f32[2,1,2048]{2,1,0:T(1,128)S(1)} %pad_maximum_fusion), channel_id=1, replica_groups=mesh['dp'=4,'tp'=16] {'tp'}, use_global_device_ids=true, to_apply=%region_6.7 | all-reduce | flops 4096 | bytes 32768 | tf_op jit(solution)/shard_map/psum | solution.py:28
  144.8 0.6 fusion.17
  145.5 0.0 copy-start
  145.5 0.0 copy-done.2
  145.5 1.2 fusion.19
  146.7 0.0 copy-done
  (5 shorter events, 0.0 us)
Async XLA Ops:
  0.6 12.3 %copy-start.3 = (f32[2560]{0:T(1024)S(1)}, f32[2560]{0:T(1024)}, u32[]{:S(2)}) copy-start(f32[2560]{0:T(1024)} %param.8) | copy-start | bytes 30724
  0.6 12.3 %copy-start.4 = (f32[2560]{0:T(1024)S(1)}, f32[2560]{0:T(1024)}, u32[]{:S(2)}) copy-start(f32[2560]{0:T(1024)} %param.7) | copy-start | bytes 30724
  13.0 75.9 %copy-start.1 = (s32[1,2048]{1,0:T(1,128)S(1)}, s32[1,2048]{1,0:T(1,128)}, u32[]{:S(2)}) copy-start(s32[1,2048]{1,0:T(1,128)} %param.10) | copy-start | bytes 24580
  59.5 85.9 %copy-start.2 = (s32[1,2048]{1,0:T(1,128)S(1)}, s32[1,2048]{1,0:T(1,128)}, u32[]{:S(2)}) copy-start(s32[1,2048]{1,0:T(1,128)} %param.11) | copy-start | bytes 24580
  145.5 1.2 copy-start
where the time goes:
time: 149 us; the launch traced here: 147 us
  blocking collectives  74.5 us (50%)
  matrix products  46.6 us (31%)
  other arithmetic  24.8 us (17%)
    dot_general x1, matrix products, local_part(): jnp.einsum('bsd,vd->bsv', normed, embedding, preferred_element_type=jnp.f...  46.6 us
    psum x1, blocking collectives, local_part(): combined = lax.psum(jnp.stack([exp_sum, target_part]), 'tp')  45.2 us
    pmax x1, blocking collectives, local_part(): row_max = lax.pmax(jnp.max(logits, axis=-1), 'tp')  29.3 us
    reduce_sum x1, other arithmetic, local_part(): exp_sum = jnp.sum(jnp.exp(logits - row_max[..., None]), axis=-1)  10.7 us
    reduce_sum x1, other arithmetic, layer_norm(): row_var = jnp.mean(centered * centered, axis=-1, keepdims=True)  6.83 us
    reduce_sum x1, other arithmetic, layer_norm(): row_mean = jnp.mean(hidden_f, axis=-1, keepdims=True)  5.41 us

commit v1 on v0

v1 whole, which is shorter than its diff:
```python
import functools

import jax
import jax.numpy as jnp
from jax import lax
from jax.experimental import pallas as pl
from jax.experimental.pallas import tpu as pltpu
from jax.sharding import PartitionSpec as P

OPT_VOCAB = 50272
LN_EPS = 1e-5
MESH = pl.DeviceIdType.MESH
TILE = 512
LANES = 128
CHUNK = 400
PIECE = 80
LNROWS = 16
LN_PLAN = (6, 6, 6, 5, 5, 4, 0, 0)
E_GROUPS = ((0, 2), (2, 4), (4, 8))


def kernel(n, x_hbm, gain_hbm, bias_hbm, e_hbm, tgt_hbm, mask_hbm, out_ref,
           x_ref, e_ref, h_ref, gain1_ref, bias1_ref, gain_ref, bias_ref, tgt_ref, mask_ref, m_ref, s_ref, t_ref, comm_ref,
           x_sem, e_sem, small_sem, send_sem, recv_sem, *, seq, vocab, depth):
    ntile = seq // TILE
    nchunk = vocab // CHUNK
    me = lax.axis_index("tp")

    def x_copy(b):
        rows = pl.ds(pl.multiple_of(b * TILE, TILE), TILE)
        return pltpu.make_async_copy(x_hbm.at[rows, :], x_ref.at[rows, :], x_sem.at[b])

    def e_copy(g):
        first, last = E_GROUPS[g]
        rows = pl.ds(first * CHUNK, (last - first) * CHUNK)
        return pltpu.make_async_copy(e_hbm.at[rows, :], e_ref.at[rows, :], e_sem.at[g])

    small = [pltpu.make_async_copy(src, dst, small_sem.at[i]) for i, (src, dst) in enumerate(
        ((gain_hbm, gain1_ref), (bias_hbm, bias1_ref), (tgt_hbm, tgt_ref), (mask_hbm, mask_ref)))]
    for copy in small[:2]:
        copy.start()
    x_copy(0).start()
    e_copy(0).start()
    for copy in small[2:]:
        copy.start()
    e_copy(1).start()
    x_copy(1).start()
    e_copy(2).start()
    for b in range(2, ntile):
        x_copy(b).start()

    barrier = pltpu.get_barrier_semaphore()
    for d in range(1, n):
        pl.semaphore_signal(barrier, inc=1, device_id={"tp": lax.rem(me + d, n)}, device_id_type=MESH)

    m_ref[...] = jnp.full_like(m_ref, -jnp.inf)
    s_ref[...] = jnp.zeros_like(s_ref)
    t_ref[...] = jnp.zeros_like(t_ref)
    small[0].wait()
    small[1].wait()
    gain_ref[...] = gain1_ref[...].reshape(1, depth)
    bias_ref[...] = bias1_ref[...].reshape(1, depth)

    def norm_block(row, slot, hrow):
        x = x_ref[pl.ds(row, LNROWS), :].astype(jnp.float32)
        mean = jnp.sum(x, axis=-1, keepdims=True) * (1.0 / depth)
        centered = x - mean
        var = jnp.sum(centered * centered, axis=-1, keepdims=True) * (1.0 / depth)
        y = centered * lax.rsqrt(var + LN_EPS) * gain_ref[...] + bias_ref[...]
        h_ref[slot, pl.ds(hrow, LNROWS), :] = y.astype(jnp.bfloat16)

    x_copy(0).wait()

    def first_norm(j, carry):
        for q in range(8):
            row = pl.multiple_of(j * (8 * LNROWS) + q * LNROWS, LNROWS)
            norm_block(row, 0, row)
        return carry

    lax.fori_loop(0, TILE // (8 * LNROWS), first_norm, 0)
    small[2].wait()
    small[3].wait()

    nvalid = OPT_VOCAB - me * vocab
    sub = lax.broadcasted_iota(jnp.int32, (8, TILE), 0)

    def update(z, tile, base):
        m, total, hit = m_ref[tile], s_ref[tile], t_ref[tile]
        tgt = tgt_ref[0:1, pl.ds(pl.multiple_of(tile * TILE, TILE), TILE)]
        rel = (tgt - me * vocab - base) - sub
        for q in range(0, CHUNK, PIECE):
            v = [z[r:r + 8] for r in range(q, q + PIECE, 8)]
            v = [a + jnp.where(base + q + 8 * j < nvalid, 0.0, -jnp.inf) for j, a in enumerate(v)]
            m_new = functools.reduce(jnp.maximum, v, m)
            total = total * jnp.exp(m - m_new)
            for a in v:
                total += jnp.exp(a - m_new)
            m = m_new
            for j, a in enumerate(v):
                hit = jnp.where(rel == q + 8 * j, a, hit)
        m_ref[tile], s_ref[tile], t_ref[tile] = m, total, hit

    def run_tile(tile, slot, nxt, first):
        blk = 0
        for c in range(nchunk):
            if first:
                for g, (start, _) in enumerate(E_GROUPS):
                    if start == c:
                        e_copy(g).wait()
            e = e_ref[c * CHUNK:(c + 1) * CHUNK, :]
            z = lax.dot_general(e, h_ref[slot], (((1,), (1,)), ((), ())), preferred_element_type=jnp.float32)
            update(z, tile, c * CHUNK)
            for _ in range(LN_PLAN[c]):
                row = blk * LNROWS
                norm_block(pl.multiple_of(nxt * TILE + row, LNROWS), 1 - slot, row)
                blk += 1

    def send(tile, d):
        return pltpu.make_async_remote_copy(
            src_ref=comm_ref.at[tile, me], dst_ref=comm_ref.at[tile, me],
            send_sem=send_sem.at[tile, d], recv_sem=recv_sem.at[tile, d],
            device_id={"tp": lax.rem(me + d, n)}, device_id_type=MESH)

    def finish_tile(tile):
        m = m_ref[tile]
        top = jnp.max(m, axis=0, keepdims=True)
        total = jnp.sum(s_ref[tile] * jnp.exp(m - top), axis=0, keepdims=True)
        hit = jnp.sum(t_ref[tile], axis=0, keepdims=True)
        for g, v in enumerate((top, total, hit)):
            for j in range(TILE // LANES):
                r = g * (TILE // LANES) + j
                comm_ref[tile, me, r:r + 1, :] = v[:, j * LANES:(j + 1) * LANES]
        for d in range(1, n):
            send(tile, d).start()

    x_copy(1).wait()
    run_tile(0, 0, 1, True)
    pl.semaphore_wait(barrier, n - 1)
    finish_tile(0)

    def step(tile, carry):
        @pl.when(tile < ntile - 1)
        def _():
            x_copy(tile + 1).wait()

        run_tile(tile, lax.rem(tile, 2), jnp.minimum(tile + 1, ntile - 1), False)
        finish_tile(tile)
        return carry

    lax.fori_loop(1, ntile, step, 0)

    rows_t = TILE // LANES
    rows_o = seq // LANES
    acc = jnp.zeros((rows_t, LANES), jnp.float32)
    for tile in range(ntile):
        for d in range(1, n):
            send(tile, d).wait_recv()
        tops = [comm_ref[tile, p, 0:rows_t, :] for p in range(n)]
        top = functools.reduce(jnp.maximum, tops)
        total = sum(comm_ref[tile, p, rows_t:2 * rows_t, :] * jnp.exp(tops[p] - top) for p in range(n))
        hit = sum(comm_ref[tile, p, 2 * rows_t:3 * rows_t, :] for p in range(n))
        rows = slice(tile * rows_t, (tile + 1) * rows_t)
        logn = top + jnp.log(total)
        tok = (hit - logn) * mask_ref[rows, :].astype(jnp.float32)
        acc += tok
        for g, v in enumerate((logn, tok, top - logn)):
            out_ref[g * rows_o + tile * rows_t:g * rows_o + (tile + 1) * rows_t, :] = v
    acc = jnp.sum(jnp.sum(acc, axis=0, keepdims=True), axis=1, keepdims=True)
    out_ref[3 * rows_o:3 * rows_o + 8, :] = jnp.broadcast_to(acc, (8, LANES))
    for tile in range(ntile):
        for d in range(1, n):
            send(tile, d).wait_send()


def solution(mesh):
    n = mesh.shape["tp"]

    def local_part(hidden, ln_gain, ln_bias, embedding, targets, score_mask):
        batch, seq, depth = hidden.shape
        vocab = embedding.shape[0]
        ntile = seq // TILE
        rows = seq // LANES
        hbm = pl.BlockSpec(memory_space=pltpu.HBM)
        state = pltpu.VMEM((ntile, 8, TILE), jnp.float32)
        out = pl.pallas_call(
            functools.partial(kernel, n, seq=seq, vocab=vocab, depth=depth),
            out_shape=jax.ShapeDtypeStruct((3 * rows + 8, LANES), jnp.float32),
            in_specs=[hbm] * 6,
            out_specs=pl.BlockSpec(memory_space=pltpu.VMEM),
            scratch_shapes=[
                pltpu.VMEM((seq, depth), jnp.bfloat16),
                pltpu.VMEM((vocab, depth), jnp.bfloat16),
                pltpu.VMEM((2, TILE, depth), jnp.bfloat16),
                pltpu.VMEM((depth,), jnp.float32),
                pltpu.VMEM((depth,), jnp.float32),
                pltpu.VMEM((1, depth), jnp.float32),
                pltpu.VMEM((1, depth), jnp.float32),
                pltpu.VMEM((1, seq), jnp.int32),
                pltpu.VMEM((rows, LANES), jnp.int32),
                state, state, state,
                pltpu.VMEM((ntile, n, 3 * TILE // LANES, LANES), jnp.float32),
                pltpu.SemaphoreType.DMA((ntile,)),
                pltpu.SemaphoreType.DMA((len(E_GROUPS),)),
                pltpu.SemaphoreType.DMA((4,)),
                pltpu.SemaphoreType.DMA((ntile, n)),
                pltpu.SemaphoreType.DMA((ntile, n)),
            ],
            compiler_params=pltpu.CompilerParams(collective_id=0, has_side_effects=True,
                                                 vmem_limit_bytes=61 * 1024 * 1024),
            name="score",
        )(hidden.reshape(batch * seq, depth), ln_gain, ln_bias, embedding,
          targets.reshape(1, seq), score_mask.reshape(rows, LANES))
        logn, tok, top = (out[g * rows:(g + 1) * rows].reshape(1, seq) for g in range(3))
        return logn, tok, out[3 * rows, 0:1], top

    row_spec = P("dp", None)
    return jax.shard_map(local_part, mesh=mesh, in_specs=(P("dp", None, None), P(), P(), P("tp", None), row_spec, row_spec), out_specs=(row_spec, row_spec, P("dp"), row_spec), check_vma=False)
```

time: 149 us -> 63.5 us (0.43); the launches traced: 147 us -> 63.2 us
  blocking collectives: 74.5 us -> 0 us
  Pallas kernels: 0 us -> 60 us
  matrix products: 46.6 us -> 0 us
  other arithmetic: 24.8 us -> 0 us
  local copies, waits for them, and re-layouts: 0.02 us -> 2.53 us
    pallas_call x0 -> x1, Pallas kernels: none -> 60 us  [local_part(): pl.pallas_call(functools.partial(kernel, n, seq=seq, vocab=vocab, depth=d...]
    dot_general x1 -> x0, matrix products: 46.6 us -> none  [local_part(): jnp.einsum('bsd,vd->bsv', normed, embedding, preferred_element_type=jnp.f...]
    psum x1 -> x0, blocking collectives: 45.2 us -> none  [local_part(): combined = lax.psum(jnp.stack([exp_sum, target_part]), 'tp')]
    pmax x1 -> x0, blocking collectives: 29.3 us -> none  [local_part(): row_max = lax.pmax(jnp.max(logits, axis=-1), 'tp')]
    reduce_sum x4 -> x0, other arithmetic: 24.2 us -> none  [the longest x1 10.7 us: local_part(): exp_sum = jnp.sum(jnp.exp(logits - row_max[..., None]), axis=-1)]
    slice x0 -> x2, local copies, waits for them, and re-layouts: none -> 2.53 us  [the longest x1 1.34 us: local_part(): out[g * rows:(g + 1) * rows].reshape(1, seq)]
where the time goes in v1:
time: 63.5 us; the launch traced here: 63.2 us
  Pallas kernels  60 us (94%)
  local copies, waits for them, and re-layouts  2.53 us (4%)
  between operations  0.64 us (1%)
    pallas_call x1, Pallas kernels, local_part(): pl.pallas_call(functools.partial(kernel, n, seq=seq, vocab=vocab, depth=d...  60 us
    slice x1, local copies, waits for them, and re-layouts, local_part(): out[g * rows:(g + 1) * rows].reshape(1, seq)  1.34 us

profile of v1, /device:TPU:21, one launch (start us, length us, event | category | flops | bytes accessed | tf_op | source)
XLA Modules:
  0.0 63.2 jit_solution(17263673739337974551)
XLA Ops:
  0.6 60.0 %score.1 = f32[56,128]{1,0:T(8,128)} custom-call(bf16[2048,2560]{1,0:T(8,128)(2,1)} %bitcast.6, f32[2560]{0:T(1024)} %gain_hbm.1, f32[2560]{0:T(1024)} %bias_hbm.1, bf16[3200,2560]{1,0:T(8,128)(2,1)} %e_hbm.1, s32[1,2048]{1,0:T(1,128)} %tgt_hbm.1, s32[16,128]{1,0:T(8,128)} %bitcast.7), custom_call_target="tpu_custom_call" | custom-call | tf_op jit(solution)/shard_map/score/pallas_call | solution.py:185
  60.7 1.3 %fusion = (f32[16,128]{1,0:T(8,128)}, f32[16,128]{1,0:T(8,128)}, f32[16,128]{1,0:T(8,128)}) fusion(f32[56,128]{1,0:T(8,128)} %score.1), kind=kLoop, calls=%fused_computation | loop fusion | bytes 49152 | tf_op jit(solution)/shard_map/slice | solution.py:213
  62.0 1.2 %slice.14 = f32[1,1]{1,0:T(1,128)} slice(f32[56,128]{1,0:T(8,128)} %score.1), slice={[48:49], [0:1]} | slice | bytes 8 | tf_op jit(solution)/shard_map/slice | solution.py:214

commit v2 on v1

v2 whole, which is shorter than its diff:
```python
import functools

import jax
import jax.numpy as jnp
from jax import lax
from jax.experimental import pallas as pl
from jax.experimental.pallas import tpu as pltpu
from jax.sharding import PartitionSpec as P

OPT_VOCAB = 50272
LN_EPS = 1e-5
MESH = pl.DeviceIdType.MESH
TILE = 512
LANES = 128
CHUNK = 320
PIECE = 80
LG = 256
LNROWS = 16
XROWS = 128
LN_FIRST = (0, 4, 4, 4, 4, 4, 4, 4, 4, 0)
LN_PLAN = (4, 4, 4, 4, 4, 3, 3, 3, 3, 0)
E_GROUPS = ((0, 2), (2, 5), (5, 10))
UNROLL = False


def kernel(n, x_hbm, gain_hbm, bias_hbm, e_hbm, tgt_hbm, mask_hbm, out_ref,
           x_ref, e_ref, h_ref, gain1_ref, bias1_ref, gain_ref, bias_ref, tgt_ref, mask_ref, m_ref, s_ref, t_ref, comm_ref,
           x_sem, e_sem, small_sem, send_sem, recv_sem, *, seq, vocab, depth):
    ntile = seq // TILE
    nchunk = vocab // CHUNK
    nblk = TILE // XROWS
    me = lax.axis_index("tp")
    zero = me - 2 * lax.div(me, 2) - lax.rem(me, 2)

    def x_copy(first, count, sem):
        rows = pl.ds(first, count)
        return pltpu.make_async_copy(x_hbm.at[rows, :], x_ref.at[rows, :], x_sem.at[sem])

    def x_block(b):
        return x_copy(pl.multiple_of(b * XROWS, XROWS), XROWS, b)

    def x_tile(t):
        return x_copy(pl.multiple_of(t * TILE, TILE), TILE, nblk + t)

    def e_copy(g):
        first, last = E_GROUPS[g]
        rows = pl.ds(first * CHUNK, (last - first) * CHUNK)
        return pltpu.make_async_copy(e_hbm.at[rows, :], e_ref.at[rows, :], e_sem.at[g])

    small = [pltpu.make_async_copy(src, dst, small_sem.at[i]) for i, (src, dst) in enumerate(
        ((gain_hbm, gain1_ref), (bias_hbm, bias1_ref), (tgt_hbm, tgt_ref), (mask_hbm, mask_ref)))]
    x_block(0).start()
    for copy in small:
        copy.start()
    for b in range(1, nblk):
        x_block(b).start()
    e_copy(0).start(priority=1)
    e_copy(1).start(priority=1)
    x_tile(1).start(priority=1)
    for g in range(2, len(E_GROUPS)):
        e_copy(g).start(priority=1)
    for t in range(2, ntile):
        x_tile(t).start(priority=1)

    def peer(d):
        return {"tp": jnp.bitwise_xor(me, d)}

    barrier = pltpu.get_barrier_semaphore()
    for d in range(1, n):
        pl.semaphore_signal(barrier, inc=1, device_id=peer(d), device_id_type=MESH)

    m_ref[...] = jnp.full_like(m_ref, -jnp.inf)
    s_ref[...] = jnp.zeros_like(s_ref)
    t_ref[...] = jnp.zeros_like(t_ref)
    small[0].wait()
    small[1].wait()
    gain_ref[...] = gain1_ref[...].reshape(1, depth)
    bias_ref[...] = bias1_ref[...].reshape(1, depth)

    def norm_block(row, slot, hrow):
        x = x_ref[pl.ds(row, LNROWS), :].astype(jnp.float32)
        mean = jnp.sum(x, axis=-1, keepdims=True) * (1.0 / depth)
        centered = x - mean
        var = jnp.sum(centered * centered, axis=-1, keepdims=True) * (1.0 / depth)
        y = centered * lax.rsqrt(var + LN_EPS) * gain_ref[...] + bias_ref[...]
        h_ref[slot, pl.ds(hrow, LNROWS), :] = y.astype(jnp.bfloat16)

    def first_norm(j, carry):
        x_block(j).wait()
        for q in range(0, XROWS, LNROWS):
            row = pl.multiple_of(j * XROWS + q, LNROWS)
            norm_block(row, 0, row)
        return carry

    lax.fori_loop(0, nblk, first_norm, 0)
    small[2].wait()
    small[3].wait()

    nvalid = OPT_VOCAB - me * vocab
    min_valid = OPT_VOCAB - (n - 1) * vocab
    sub = lax.broadcasted_iota(jnp.int32, (8, LG), 0)

    def padded(v, row, base):
        return v if row < min_valid else v + jnp.where(row < nvalid, 0.0, -jnp.inf)

    def update(z, tile, base):
        for u in range(0, TILE, LG):
            cols = slice(u, u + LG)
            m, total, hit = m_ref[tile, :, cols], s_ref[tile, :, cols], t_ref[tile, :, cols]
            tgt = tgt_ref[0:1, pl.ds(pl.multiple_of(tile * TILE + u, LG), LG)]
            rel = (tgt - me * vocab - base) - sub
            for q in range(0, CHUNK, PIECE):
                v = [padded(z[r:r + 8, cols], base + r, base) for r in range(q, q + PIECE, 8)]
                m_new = functools.reduce(jnp.maximum, v, m)
                total = total * jnp.exp(m - m_new)
                for a in v:
                    total += jnp.exp(a - m_new)
                m = m_new
                for j, a in enumerate(v):
                    hit = jnp.where(rel == q + 8 * j, a, hit)
            m_ref[tile, :, cols], s_ref[tile, :, cols], t_ref[tile, :, cols] = m, total, hit

    def run_tile(tile, slot, nxt, first, plan):
        blk = 0
        for c in range(nchunk):
            if first:
                for g, (start, _) in enumerate(E_GROUPS):
                    if start == c:
                        e_copy(g).wait()
                if c == 1:
                    x_tile(1).wait()
            e = e_ref[c * CHUNK:(c + 1) * CHUNK, :]
            z = lax.dot_general(e, h_ref[slot], (((1,), (1,)), ((), ())), preferred_element_type=jnp.float32)
            update(z, tile, c * CHUNK)
            for _ in range(plan[c]):
                row = blk * LNROWS
                norm_block(pl.multiple_of(nxt * TILE + row, LNROWS), 1 - slot, row)
                blk += 1

    def finish_tile(tile):
        m = m_ref[tile]
        top = jnp.max(m, axis=0, keepdims=True)
        total = jnp.sum(s_ref[tile] * jnp.exp(m - top), axis=0, keepdims=True)
        hit = jnp.sum(t_ref[tile], axis=0, keepdims=True)
        for g, v in enumerate((top, total, hit)):
            for j in range(TILE // LANES):
                r = g * (TILE // LANES) + j
                comm_ref[me, tile, r:r + 1, :] = v[:, j * LANES:(j + 1) * LANES]

    rounds = (pl.ds(0, ntile - 1), pl.ds(ntile - 1, 1))

    def send(r, d):
        return pltpu.make_async_remote_copy(
            src_ref=comm_ref.at[me, rounds[r]], dst_ref=comm_ref.at[me, rounds[r]],
            send_sem=send_sem.at[r, d], recv_sem=recv_sem.at[r, d],
            device_id=peer(d), device_id_type=MESH)

    def first_round():
        pl.semaphore_wait(barrier, n - 1)
        for d in range(1, n):
            send(0, d).start()

    run_tile(zero, zero, zero + 1, True, LN_FIRST)
    finish_tile(0)
    if UNROLL:
        for t in range(1, ntile):
            if t == ntile - 1:
                first_round()
            else:
                x_tile(t + 1).wait()
            run_tile(zero + t, zero + t % 2, zero + t + 1, False, LN_PLAN if t < ntile - 1 else (0,) * nchunk)
            finish_tile(t)
    else:
        def step(t, carry):
            @pl.when(t < ntile - 1)
            def _():
                x_tile(t + 1).wait()

            @pl.when(t == ntile - 1)
            def _():
                first_round()

            run_tile(t, lax.rem(t, 2), jnp.minimum(t + 1, ntile - 1), False, LN_PLAN)
            finish_tile(t)
            return carry

        lax.fori_loop(1, ntile, step, 0)
    for d in range(1, n):
        send(1, d).start()

    rows_t = TILE // LANES
    rows_o = seq // LANES

    def combine(tile):
        tops = [comm_ref[p, tile, 0:rows_t, :] for p in range(n)]
        top = functools.reduce(jnp.maximum, tops)
        total = sum(comm_ref[p, tile, rows_t:2 * rows_t, :] * jnp.exp(tops[p] - top) for p in range(n))
        hit = sum(comm_ref[p, tile, 2 * rows_t:3 * rows_t, :] for p in range(n))
        rows = slice(tile * rows_t, (tile + 1) * rows_t)
        logn = top + jnp.log(total)
        tok = (hit - logn) * mask_ref[rows, :].astype(jnp.float32)
        for g, v in enumerate((logn, tok, top - logn)):
            out_ref[g * rows_o + tile * rows_t:g * rows_o + (tile + 1) * rows_t, :] = v

    for d in range(1, n):
        send(0, d).wait_recv()
    for tile in range(ntile - 1):
        combine(tile)
    for d in range(1, n):
        send(0, d).wait_send()
    for d in range(1, n):
        send(1, d).wait_recv()
    combine(ntile - 1)
    for d in range(1, n):
        send(1, d).wait_send()


def solution(mesh):
    n = mesh.shape["tp"]

    def local_part(hidden, ln_gain, ln_bias, embedding, targets, score_mask):
        batch, seq, depth = hidden.shape
        vocab = embedding.shape[0]
        ntile = seq // TILE
        rows = seq // LANES
        hbm = pl.BlockSpec(memory_space=pltpu.HBM)
        state = pltpu.VMEM((ntile, 8, TILE), jnp.float32)
        out = pl.pallas_call(
            functools.partial(kernel, n, seq=seq, vocab=vocab, depth=depth),
            out_shape=pltpu.VMEM((3 * rows, LANES), jnp.float32),
            in_specs=[hbm] * 6,
            out_specs=pl.BlockSpec(memory_space=pltpu.VMEM),
            scratch_shapes=[
                pltpu.VMEM((seq, depth), jnp.bfloat16),
                pltpu.VMEM((vocab, depth), jnp.bfloat16),
                pltpu.VMEM((2, TILE, depth), jnp.bfloat16),
                pltpu.VMEM((depth,), jnp.float32),
                pltpu.VMEM((depth,), jnp.float32),
                pltpu.VMEM((1, depth), jnp.float32),
                pltpu.VMEM((1, depth), jnp.float32),
                pltpu.VMEM((1, seq), jnp.int32),
                pltpu.VMEM((rows, LANES), jnp.int32),
                state, state, state,
                pltpu.VMEM((n, ntile, 3 * TILE // LANES, LANES), jnp.float32),
                pltpu.SemaphoreType.DMA((TILE // XROWS + ntile,)),
                pltpu.SemaphoreType.DMA((len(E_GROUPS),)),
                pltpu.SemaphoreType.DMA((4,)),
                pltpu.SemaphoreType.DMA((2, n)),
                pltpu.SemaphoreType.DMA((2, n)),
            ],
            compiler_params=pltpu.CompilerParams(collective_id=0, has_side_effects=True,
                                                 vmem_limit_bytes=61 * 1024 * 1024),
            name="score",
        )(hidden.reshape(batch * seq, depth), ln_gain, ln_bias, embedding,
          targets.reshape(1, seq), score_mask.reshape(rows, LANES))
        logn, tok, top = (out[g * rows:(g + 1) * rows].reshape(1, seq) for g in range(3))
        return logn, tok, jnp.sum(tok, axis=-1), top

    row_spec = P("dp", None)
    return jax.shard_map(local_part, mesh=mesh, in_specs=(P("dp", None, None), P(), P(), P("tp", None), row_spec, row_spec), out_specs=(row_spec, row_spec, P("dp"), row_spec), check_vma=False)
```

time: 63.5 us -> 58.3 us (0.918)
  Pallas kernels: 60 us -> 56.4 us
  local copies, waits for them, and re-layouts: 2.53 us -> 0 us
  other arithmetic: 0 us -> 1.21 us
    pallas_call x1, Pallas kernels: 60 us -> 56.4 us  [local_part(): pl.pallas_call(functools.partial(kernel, n, seq=seq, vocab=vocab, depth=d...]
    slice x2 -> x0, local copies, waits for them, and re-layouts: 2.53 us -> none  [the longest x1 1.34 us: local_part(): out[g * rows:(g + 1) * rows].reshape(1, seq)]
    slice x0 -> x1, other arithmetic: none -> 1.21 us  [local_part(): out[g * rows:(g + 1) * rows].reshape(1, seq)]
where the time goes in v2:
time: 58.3 us; the launch traced here: 58.2 us
  Pallas kernels  56.4 us (97%)
  other arithmetic  1.21 us (2%)
  between operations  0.64 us (1%)
    pallas_call x1, Pallas kernels, local_part(): pl.pallas_call(functools.partial(kernel, n, seq=seq, vocab=vocab, depth=d...  56.4 us
    slice x1, other arithmetic, local_part(): out[g * rows:(g + 1) * rows].reshape(1, seq)  1.21 us

profile of v2, /device:TPU:21, one launch (start us, length us, event | category | flops | bytes accessed | tf_op | source)
XLA Modules:
  0.0 58.2 jit_solution(3013922706411737352)
XLA Ops:
  0.6 56.4 %score.1 = f32[48,128]{1,0:T(8,128)S(1)} custom-call(bf16[2048,2560]{1,0:T(8,128)(2,1)} %bitcast.6, f32[2560]{0:T(1024)} %gain_hbm.1, f32[2560]{0:T(1024)} %bias_hbm.1, bf16[3200,2560]{1,0:T(8,128)(2,1)} %e_hbm.1, s32[1,2048]{1,0:T(1,128)} %tgt_hbm.1, s32[16,128]{1,0:T(8,128)} %bitcast.7), custom_call_target="tpu_custom_call" | custom-call | tf_op jit(solution)/shard_map/score/pallas_call | solution.py:228
  57.0 1.2 %fusion = (f32[16,128]{1,0:T(8,128)}, f32[]{:T(128)}, f32[16,128]{1,0:T(8,128)}, f32[16,128]{1,0:T(8,128)}) fusion(f32[48,128]{1,0:T(8,128)S(1)} %score.1), kind=kLoop, calls=%fused_computation.1 | loop fusion | flops 2047 | bytes 49156 | tf_op jit(solution)/shard_map/slice | solution.py:256
